TPU v7x, 32 devices: a whole 2x2x4 slice. The times are simulated.
32 devices in a mesh: row: 8 (over z, core), col: 4 (over y, x).
Axes of the slice: x: 2, y: 2, z: 4, core: 2. Of those that a mesh axis runs over, the one named last changes fastest.
Arguments:
- energy: float32 [4, 2048, 2048], P('col', 'row'), may hold values from 0.5 to 8
- damage_old: float32 [4, 2048, 2048], P('col', 'row'), may hold values from 0 to 0.8
- crack_seeds: int32 [4, 2048, 2048], P('col', 'row'), may hold values 0 or 1
- irreversible: int32 [4, 2048, 2048], P('col', 'row'), may hold values 0 or 1
- line_inverses: float32 [8, 256, 256], replicated, may hold values from -0.6 to 2.8
- z_inverse: float32 [4, 4], replicated, may hold values from -0.8 to 1.9
Outputs:
- damage: float32 [4, 2048, 2048], P('col', 'row')
- update_norms: float32 [2], replicated
All inputs are finite; a program needn't handle non-finite values. No bound on the sum of `crack_seeds` or of `irreversible` on one device may be relied on, other than what follows from the above.
Results may differ from a plain program's by a relative error of at most 0.0001.
Values sent between devices are 32-bit elements; how exact they have to be, the bound alone decides.
A program may use at most 128 MiB of HBM per device.

v0:
```python
import jax
import jax.numpy as jnp
from jax import lax
from jax.sharding import PartitionSpec as P

ITERS = 2


KAPPA = 2.0
STEP = 0.02
COUPLE = 0.5
EPSILON = 1e-06


def second_difference(grid_field, along):
    extent = grid_field.shape[along]
    forward_diff = lax.slice_in_dim(grid_field, 1, extent, axis=along) - lax.slice_in_dim(
        grid_field, 0, extent - 1, axis=along
    )
    zero_shape = list(grid_field.shape)
    zero_shape[along] = 1
    zero_rim = jnp.zeros(zero_shape, grid_field.dtype)
    ahead = jnp.concatenate([forward_diff, zero_rim], axis=along)
    behind = jnp.concatenate([zero_rim, forward_diff], axis=along)
    return ahead - behind


def line_solve(line_rows, inverses):
    block_count, block_cells, _ = inverses.shape
    line_count = line_rows.shape[0]
    blocks = line_rows.reshape(line_count, block_count, block_cells)
    products = jnp.einsum("rkb,kcb->rkc", blocks, inverses, precision=lax.Precision.HIGHEST)
    first_col = inverses[:, :, 0]
    last_col = inverses[:, :, block_cells - 1]
    incoming = [jnp.zeros((line_count,), line_rows.dtype)]
    for block_index in range(block_count - 1):
        incoming.append(
            products[:, block_index, block_cells - 1]
            + COUPLE * incoming[block_index] * inverses[block_index, block_cells - 1, 0]
        )
    inflow = jnp.stack(incoming, axis=1)
    forward = products + COUPLE * inflow[:, :, None] * first_col[None]
    head_terms = [jnp.zeros((line_count,), line_rows.dtype) for block_index in range(block_count)]
    carried = forward[:, block_count - 1, 0]
    for block_index in range(block_count - 2, -1, -1):
        head_terms[block_index] = carried
        carried = (
            forward[:, block_index, 0]
            + COUPLE * carried * inverses[block_index, 0, block_cells - 1]
        )
    outflow = jnp.stack(head_terms, axis=1)
    solved = forward + COUPLE * outflow[:, :, None] * last_col[None]
    return solved.reshape(line_count, block_count * block_cells)


def local(energy, damage_old, crack_seeds, irreversible, line_inverses, z_inverse):
    planes, rows_here, line_length = energy.shape
    row_count = lax.axis_size("row")
    col_count = lax.axis_size("col")
    total_planes = planes * col_count
    cell_count = total_planes * rows_here * row_count * line_length
    seeded = crack_seeds == 1
    damage = jnp.where(seeded, 1.0, damage_old)
    lower_bound = jnp.where(irreversible == 1, damage_old, 0.0)
    own_sums = []
    for sweep_index in range(ITERS):
        local_lap = second_difference(damage, 2)
        partial_value = energy - (1.0 + energy) * damage + KAPPA * local_lap
        moved_part, moved_damage = (
            lax.all_to_all(
                lax.all_to_all(
                    jnp.swapaxes(partial_value, 1, 2),
                    "row",
                    split_axis=1,
                    concat_axis=2,
                    tiled=True,
                ),
                "col",
                split_axis=1,
                concat_axis=0,
                tiled=True,
            ),
            lax.all_to_all(
                lax.all_to_all(
                    jnp.swapaxes(damage, 1, 2), "row", split_axis=1, concat_axis=2, tiled=True
                ),
                "col",
                split_axis=1,
                concat_axis=0,
                tiled=True,
            ),
        )
        lap_rest = second_difference(moved_damage, 2) + second_difference(moved_damage, 0)
        turned = moved_part + KAPPA * lap_rest
        turned_shape = turned.shape
        along_y = line_solve(turned.reshape(-1, turned_shape[2]), line_inverses).reshape(
            turned_shape
        )
        along_z = jnp.einsum("zk,kxy->zxy", z_inverse, along_y, precision=lax.Precision.HIGHEST)
        gathered = lax.all_to_all(
            lax.all_to_all(along_z, "row", split_axis=2, concat_axis=1, tiled=True),
            "col",
            split_axis=0,
            concat_axis=1,
            tiled=True,
        )
        piece_cells = gathered.shape[1] // (row_count * col_count)
        reordered = gathered.reshape(planes, col_count, row_count, piece_cells, rows_here)
        restored = jnp.transpose(reordered, (0, 4, 2, 1, 3)).reshape(planes, rows_here, line_length)
        update = STEP * line_solve(restored.reshape(-1, line_length), line_inverses).reshape(
            restored.shape
        )
        clamped = jnp.minimum(jnp.maximum(damage + update, lower_bound), 1.0)
        renewed = jnp.where(seeded, 1.0, clamped)
        own_sum = jnp.sum((renewed - damage) ** 2)
        own_sums.append(own_sum)
        damage = renewed
    global_sums = lax.psum(jnp.stack(own_sums), ("row", "col"))
    update_norms = jnp.sqrt(global_sums / cell_count + EPSILON) / STEP
    return (damage, update_norms)


def solution(mesh):
    return jax.shard_map(
        local,
        mesh=mesh,
        in_specs=(
            P("col", "row", None),
            P("col", "row", None),
            P("col", "row", None),
            P("col", "row", None),
            P(),
            P(),
        ),
        out_specs=(P("col", "row", None), P()),
        check_vma=False,
    )
```

profile of v0, /device:TPU:0, one launch (start us, length us, event | category | flops | bytes accessed | tf_op | source)
XLA Modules:
  0.0 739.0 jit_solution(10383993715968311955)
XLA Ops:
  33.9 7.5 %add_bitcast_fusion.1 = f32[1,2048,256]{2,0,1:T(1,128)} fusion(f32[1,256,2047]{1,0,2:T(1,128)S(1)} %slice_subtract_fusion.3, f32[1,256,2048]{1,0,2:T(1,128)S(1)} %copy.151, f32[1,256,2048]{1,0,2:T(1,128)} %broadcast_select_fusion.1), kind=kLoop, calls=%fused_computation.27 | loop fusion | flops 3145728 | bytes 8387584 | tf_op jit(solution)/shard_map/transpose | solution.py:72
  41.4 32.0 %all-to-all-done.2 = f32[1,2048,256]{2,0,1:T(1,128)} async-done(((f32[1,2048,256]{2,0,1:T(1,128)}), f32[1,2048,256]{2,0,1:T(1,128)}, u32[]{:S(2)}, u32[]{:S(2)}) %all-to-all-start.2) | async-done | bytes 2097184 | tf_op jit(solution)/shard_map/all_to_all | solution.py:84
  87.5 39.3 %all-to-all-done = f32[1,2048,256]{2,0,1:T(1,128)} async-done(((f32[1,2048,256]{2,0,1:T(1,128)}), f32[1,2048,256]{2,0,1:T(1,128)}, u32[]{:S(2)}, u32[]{:S(2)}) %all-to-all-start) | async-done | bytes 2097184 | tf_op jit(solution)/shard_map/all_to_all | solution.py:71
  172.2 13.4 %all-to-all-done.1 = f32[1,256,2048]{2,0,1:T(1,128)} async-done(((f32[1,256,2048]{2,0,1:T(1,128)}), f32[1,256,2048]{2,0,1:T(1,128)}, u32[]{:S(2)}, u32[]{:S(2)}) %all-to-all-start.1) | async-done | bytes 2097184 | tf_op jit(solution)/shard_map/all_to_all | solution.py:70
  209.7 6.8 convolution_bitcast_fusion.1
  221.2 7.9 %reshape.1081 = f32[8,1,65536]{2,1,0:T(1,128)} reshape(f32[2048,4,64]{2,1,0:T(4,128)} %bitcast.194) | data formatting | bytes 4194304
  229.1 53.6 %all_to_all.174 = f32[8,1,65536]{2,1,0:T(1,128)} all-to-all(f32[8,1,65536]{2,1,0:T(1,128)} %reshape.1081), channel_id=1, replica_groups=mesh['row'=8,'col'=4] {'row'}, dimensions={0} | all-to-all | bytes 4194304 | tf_op jit(solution)/shard_map/all_to_all | solution.py:101
  283.2 8.6 %reduce = f32[8,65536]{1,0:T(8,128)} reduce(f32[8,1,65536]{2,1,0:T(1,128)} %all_to_all.174, f32[]{:T(128)} %broadcast.872), dimensions={1}, to_apply=%all_to_all.140.reduce_sub_computation | reduce | bytes 4194308 | tf_op jit(solution)/shard_map/all_to_all | solution.py:101
  291.8 6.4 reshape.1082
  314.6 18.0 %all-to-all-done.5 = f32[4,512,256]{2,1,0:T(8,128)} async-done(((f32[4,512,256]{2,1,0:T(8,128)}), f32[4,512,256]{2,1,0:T(8,128)}, u32[]{:S(2)}, u32[]{:S(2)}) %all-to-all-start.5) | async-done | bytes 2097184 | tf_op jit(solution)/shard_map/all_to_all | solution.py:100
  343.1 13.5 %minimum_select_fusion.1 = f32[1,256,2048]{1,0,2:T(1,128)} fusion(f32[1,256,2048]{1,0,2:T(1,128)} %broadcast_select_fusion.1, f32[1,256,2048]{1,2,0:T(8,128)S(1)} %bitcast.215, s32[1,256,2048]{1,0,2:T(1,128)S(1)} %copy-done.3, pred[1,256,2048]{1,0,2:T(4,128)(4,1)} %copy.170, f32[1,256,2048]{1,0,2:T(1,128)S(1)} %copy-done.5), kind=kLoop, calls=%fused_computation.21 | loop fusion | flops 3145728 | bytes 11010048 | tf_op jit(solution)/shard_map/jit(_where)/select_n | solution.py:114
  365.2 6.6 add_bitcast_fusion
  371.8 38.1 %all-to-all-done.8 = f32[1,2048,256]{2,0,1:T(1,128)} async-done(((f32[1,2048,256]{2,0,1:T(1,128)}), f32[1,2048,256]{2,0,1:T(1,128)}, u32[]{:S(2)}, u32[]{:S(2)}) %all-to-all-start.8) | async-done | bytes 2097184 | tf_op jit(solution)/shard_map/all_to_all | solution.py:84
  426.4 37.0 %all-to-all-done.6 = f32[1,2048,256]{2,0,1:T(1,128)} async-done(((f32[1,2048,256]{2,0,1:T(1,128)}), f32[1,2048,256]{2,0,1:T(1,128)}, u32[]{:S(2)}, u32[]{:S(2)}) %all-to-all-start.6) | async-done | bytes 2097184 | tf_op jit(solution)/shard_map/all_to_all | solution.py:71
  479.8 12.9 %all-to-all-done.9 = f32[1,256,2048]{2,0,1:T(1,128)} async-done(((f32[1,256,2048]{2,0,1:T(1,128)}), f32[1,256,2048]{2,0,1:T(1,128)}, u32[]{:S(2)}, u32[]{:S(2)}) %all-to-all-start.9) | async-done | bytes 2097184 | tf_op jit(solution)/shard_map/all_to_all | solution.py:83
  508.4 13.4 %all-to-all-done.7 = f32[1,256,2048]{2,0,1:T(1,128)} async-done(((f32[1,256,2048]{2,0,1:T(1,128)}), f32[1,256,2048]{2,0,1:T(1,128)}, u32[]{:S(2)}, u32[]{:S(2)}) %all-to-all-start.7) | async-done | bytes 2097184 | tf_op jit(solution)/shard_map/all_to_all | solution.py:70
  545.9 6.8 convolution_bitcast_fusion
  557.4 7.9 %reshape.1083 = f32[8,1,65536]{2,1,0:T(1,128)} reshape(f32[2048,4,64]{2,1,0:T(4,128)} %bitcast.196) | data formatting | bytes 4194304
  565.3 53.7 %all_to_all.175 = f32[8,1,65536]{2,1,0:T(1,128)} all-to-all(f32[8,1,65536]{2,1,0:T(1,128)} %reshape.1083), channel_id=1, replica_groups=mesh['row'=8,'col'=4] {'row'}, dimensions={0} | all-to-all | bytes 4194304 | tf_op jit(solution)/shard_map/all_to_all | solution.py:101
  618.9 8.5 %reduce.1 = f32[8,65536]{1,0:T(8,128)} reduce(f32[8,1,65536]{2,1,0:T(1,128)} %all_to_all.175, f32[]{:T(128)} %broadcast.872), dimensions={1}, to_apply=%all_to_all.157.reduce_sub_computation | reduce | bytes 4194308 | tf_op jit(solution)/shard_map/all_to_all | solution.py:101
  627.4 6.4 reshape.1084
  638.6 29.1 %all_to_all.176 = f32[4,512,256]{2,1,0:T(8,128)S(1)} all-to-all(f32[4,512,256]{2,1,0:T(8,128)} %bitcast.202), channel_id=1, replica_groups=mesh['row'=8,'col'=4] {'col'}, dimensions={0} | all-to-all | bytes 4194304 | tf_op jit(solution)/shard_map/all_to_all | solution.py:100
  676.6 16.7 %multiply_reduce_fusion.1 = (f32[]{:T(128)}, f32[]{:T(128)}, f32[1,256,2048]{1,0,2:T(1,128)}) fusion(f32[1,256,2048]{1,0,2:T(1,128)} %minimum_select_fusion.1, f32[1,256,2048]{1,0,2:T(1,128)} %broadcast_select_fusion.1, pred[1,256,2048]{1,0,2:T(4,128)(4,1)} %copy.170, f32[1,256,2048]{1,0,2:T(1,128)S(1)} %copy-done.6, f32[1,256,2048]{1,2,0:T(8,128)S(1)} %bitcast.218, ...), kind=kLoop, calls=%fused_computation.13 | loop fusion | flops 6291454 | bytes 13107208 | tf_op jit(solution)/shard_map/reduce_sum | solution.py:115
  694.6 37.3 %psum.7 = f32[2]{0:T(128)S(1)} all-reduce(f32[2]{0:T(128)S(1)} %pad_maximum_fusion), channel_id=1, replica_groups=mesh['row'=8,'col'=4] {'row','col'}, use_global_device_ids=true, to_apply=%region_2.3 | all-reduce | flops 2 | bytes 16 | tf_op jit(solution)/shard_map/psum | solution.py:118
  (145 shorter events, 247.9 us)
Async XLA Ops:
  0.6 209.0 %copy-start = (f32[4,4]{1,0:T(4,128)S(1)}, f32[4,4]{1,0:T(4,128)}, u32[]{:S(2)}) copy-start(f32[4,4]{1,0:T(4,128)} %param.11) | copy-start | bytes 196
  5.3 6.2 copy-start.2
  17.9 55.5 %all-to-all-start.2 = ((f32[1,2048,256]{2,0,1:T(1,128)}), f32[1,2048,256]{2,0,1:T(1,128)}, u32[]{:S(2)}, u32[]{:S(2)}) async-start(f32[1,2048,256]{2,0,1:T(1,128)} %bitcast.3), calls=%async_computation.2 | async-start | bytes 4194304 | tf_op jit(solution)/shard_map/all_to_all | solution.py:84
  29.0 4.9 copy-start.11
  73.4 53.4 %all-to-all-start = ((f32[1,2048,256]{2,0,1:T(1,128)}), f32[1,2048,256]{2,0,1:T(1,128)}, u32[]{:S(2)}, u32[]{:S(2)}) async-start(f32[1,2048,256]{2,0,1:T(1,128)} %add_bitcast_fusion.1), calls=%async_computation | async-start | bytes 4194304 | tf_op jit(solution)/shard_map/all_to_all | solution.py:71
  87.5 43.8 %copy-start.1 = (f32[8,256,256]{2,1,0:T(8,128)S(1)}, f32[8,256,256]{2,1,0:T(8,128)}, u32[]{:S(2)}) copy-start(f32[8,256,256]{2,1,0:T(8,128)} %param.10) | copy-start | bytes 6291460
  126.8 29.4 %all-to-all-start.3 = ((f32[1,256,2048]{2,0,1:T(1,128)}), f32[1,256,2048]{2,0,1:T(1,128)}, u32[]{:S(2)}, u32[]{:S(2)}) async-start(f32[1,256,2048]{2,0,1:T(1,128)} %copy.155), calls=%async_computation.3 | async-start | bytes 4194304 | tf_op jit(solution)/shard_map/all_to_all | solution.py:83
  156.2 29.4 %all-to-all-start.1 = ((f32[1,256,2048]{2,0,1:T(1,128)}), f32[1,256,2048]{2,0,1:T(1,128)}, u32[]{:S(2)}, u32[]{:S(2)}) async-start(f32[1,256,2048]{2,0,1:T(1,128)} %copy.153), calls=%async_computation.1 | async-start | bytes 4194304 | tf_op jit(solution)/shard_map/all_to_all | solution.py:70
  185.6 2.6 copy-start.13
  185.6 2.7 copy-start.15
  193.1 1.4 copy-start.8
  303.0 29.7 %all-to-all-start.5 = ((f32[4,512,256]{2,1,0:T(8,128)}), f32[4,512,256]{2,1,0:T(8,128)}, u32[]{:S(2)}, u32[]{:S(2)}) async-start(f32[4,512,256]{2,1,0:T(8,128)} %bitcast.198), calls=%async_computation.5 | async-start | bytes 4194304 | tf_op jit(solution)/shard_map/all_to_all | solution.py:100
  340.2 2.2 copy-start.3
  340.2 2.8 copy-start.5
  356.5 53.4 %all-to-all-start.8 = ((f32[1,2048,256]{2,0,1:T(1,128)}), f32[1,2048,256]{2,0,1:T(1,128)}, u32[]{:S(2)}, u32[]{:S(2)}) async-start(f32[1,2048,256]{2,0,1:T(1,128)} %bitcast.65), calls=%async_computation.8 | async-start | bytes 4194304 | tf_op jit(solution)/shard_map/all_to_all | solution.py:84
  360.9 4.3 copy-start.12
  409.9 53.4 %all-to-all-start.6 = ((f32[1,2048,256]{2,0,1:T(1,128)}), f32[1,2048,256]{2,0,1:T(1,128)}, u32[]{:S(2)}, u32[]{:S(2)}) async-start(f32[1,2048,256]{2,0,1:T(1,128)} %add_bitcast_fusion), calls=%async_computation.6 | async-start | bytes 4194304 | tf_op jit(solution)/shard_map/all_to_all | solution.py:71
  463.4 29.4 %all-to-all-start.9 = ((f32[1,256,2048]{2,0,1:T(1,128)}), f32[1,256,2048]{2,0,1:T(1,128)}, u32[]{:S(2)}, u32[]{:S(2)}) async-start(f32[1,256,2048]{2,0,1:T(1,128)} %copy.176), calls=%async_computation.9 | async-start | bytes 4194304 | tf_op jit(solution)/shard_map/all_to_all | solution.py:83
  492.7 29.1 %all-to-all-start.7 = ((f32[1,256,2048]{2,0,1:T(1,128)}), f32[1,256,2048]{2,0,1:T(1,128)}, u32[]{:S(2)}, u32[]{:S(2)}) async-start(f32[1,256,2048]{2,0,1:T(1,128)} %copy.174), calls=%async_computation.7 | async-start | bytes 4194304 | tf_op jit(solution)/shard_map/all_to_all | solution.py:70
  521.8 2.6 copy-start.14
  521.8 2.7 copy-start.16
  670.2 1.4 copy-start.7
  673.7 2.2 copy-start.4
  673.7 2.8 copy-start.6
  (2 other events, 2.7 us)
where the time goes:
time: 748 us; the launch traced here: 739 us
  waiting for transfers between devices  205 us (27%)
  local copies, waits for them, and re-layouts  174 us (23%)
  blocking collectives  174 us (23%)
  other arithmetic  110 us (15%)
  starting transfers between devices  42.7 us (6%)
  matrix products  24 us (3%)
  between operations  9.81 us (1%)
    all_to_all x2, blocking collectives, local(): lax.all_to_all(along_z, 'row', split_axis=2, concat_axis=1, tiled=True)  107 us
    unnamed x54, local copies, waits for them, and re-layouts  81.7 us
    all_to_all x2, waiting for transfers between devices, local(): lax.all_to_all(jnp.swapaxes(partial_value, 1, 2), 'row', split_axis=1, co...  76.3 us
    all_to_all x2, waiting for transfers between devices, local(): lax.all_to_all(jnp.swapaxes(damage, 1, 2), 'row', split_axis=1, concat_ax...  70.1 us
    psum x1, blocking collectives, local(): global_sums = lax.psum(jnp.stack(own_sums), ('row', 'col'))  37.3 us
    all_to_all x1, blocking collectives, local(): lax.all_to_all(lax.all_to_all(along_z, 'row', split_axis=2, concat_axis=1...  29.1 us
    all_to_all x2, waiting for transfers between devices, local(): lax.all_to_all(lax.all_to_all(jnp.swapaxes(partial_value, 1, 2), 'row', s...  26.8 us
    another operation x4, local copies, waits for them, and re-layouts, local(): line_solve(turned.reshape(-1, turned_shape[2]), line_inverses)  20.3 us
  transfers between devices with their start and end apart: 9, of which 9 were waited for; matrix products, arithmetic and copies ran while one was open for 14% of the time, Pallas kernels for 0%

commit v1 on v0

--- a/solution.py
+++ b/solution.py
@@ -1,6 +1,10 @@
+import functools
+
 import jax
 import jax.numpy as jnp
 from jax import lax
+from jax.experimental import pallas as pl
+from jax.experimental.pallas import tpu as pltpu
 from jax.sharding import PartitionSpec as P
 
 ITERS = 2
@@ -10,6 +14,7 @@
 STEP = 0.02
 COUPLE = 0.5
 EPSILON = 1e-06
+HIGHEST = lax.Precision.HIGHEST
 
 
 def second_difference(grid_field, along):
@@ -53,7 +58,7 @@
     return solved.reshape(line_count, block_count * block_cells)
 
 
-def local(energy, damage_old, crack_seeds, irreversible, line_inverses, z_inverse):
+def local_turned(energy, damage_old, crack_seeds, irreversible, line_inverses, z_inverse):
     planes, rows_here, line_length = energy.shape
     row_count = lax.axis_size("row")
     col_count = lax.axis_size("col")
@@ -120,9 +125,434 @@
     return (damage, update_norms)
 
 
+def line_kernel(
+    shape,
+    corners,
+    z_inv,
+    energy,
+    damage_old,
+    crack_seeds,
+    irreversible,
+    inverses,
+    out,
+    norms,
+    start,
+    bound,
+    ez,
+    fz,
+    dz,
+    mix,
+    gx,
+    gy,
+    gend,
+    ab_x,
+    ab_y,
+    x_send,
+    x_all,
+    h_send,
+    h_recv,
+    y_send,
+    y_all,
+    s_send,
+    s_col,
+    s_row_send,
+    s_row,
+    local_sems,
+    move_send,
+    move_recv,
+    back_send,
+    back_recv,
+    x_ssem,
+    x_rsem,
+    h_ssem,
+    h_rsem,
+    v_ssem,
+    v_rsem,
+    y_ssem,
+    y_rsem,
+    sc_ssem,
+    sc_rsem,
+    sr_ssem,
+    sr_rsem,
+):
+    rows, cols, cells, width, x_blocks, blocks, cell_count = shape
+    planes = cols
+    last = cells - 1
+    row, col = lax.axis_index("row"), lax.axis_index("col")
+    ends = 8
+    tail = 2 * x_blocks - 1
+
+    def slab(who):
+        return pl.ds(pl.multiple_of(who * width, width), width)
+
+    def send(src, dst, ssem, rsem, **where):
+        copy = pltpu.make_async_remote_copy(
+            src_ref=src, dst_ref=dst, send_sem=ssem, recv_sem=rsem,
+            device_id=where, device_id_type=pl.DeviceIdType.MESH,
+        )
+        copy.start()
+        return copy
+
+    def dot(a, b, contract):
+        return lax.dot_general(
+            a, b, (contract, ((), ())), precision=HIGHEST, preferred_element_type=jnp.float32
+        )
+
+    fetch = [
+        pltpu.make_async_copy(inverses.at[col * x_blocks + j], gx.at[j], local_sems.at[j])
+        for j in range(x_blocks)
+    ]
+    fetch.append(pltpu.make_async_copy(inverses.at[row], gy, local_sems.at[x_blocks]))
+    for copy in fetch:
+        copy.start()
+
+    moves = []
+    inside = pl.ds(8, cells)
+
+    def move(index, src, landing):
+        sent = []
+        for o in range(1, cols):
+            peer = lax.rem(col + o, cols)
+            sent.append(
+                send(src.at[:, slab(peer)], landing, move_send.at[index, o - 1],
+                     move_recv.at[index, o - 1], col=peer)
+            )
+        moves.append(sent)
+
+    move(0, energy, ez.at[col])
+
+    @pl.loop(0, cells // 16)
+    def _(i):
+        at = pl.ds(pl.multiple_of(i * 16, 16), 16)
+        old = damage_old[at, :]
+        seeded = crack_seeds[at, :] == 1
+        start[at, :] = jnp.where(seeded, 1.0, old)
+        bound[at, :] = jnp.where(seeded, 1.0, jnp.where(irreversible[at, :] == 1, old, 0.0))
+
+    ez[col] = energy[:, slab(col)]
+    move(1, start, dz.at[0, col, inside, :])
+    dz[0, col, inside, :] = start[:, slab(col)]
+    move(2, bound, fz.at[col])
+    fz[col] = bound[:, slab(col)]
+
+    lane = lax.broadcasted_iota(jnp.int32, (8, 128), 1)
+    sub = lax.broadcasted_iota(jnp.int32, (8, 128), 0)
+
+    def carries(first, own):
+        zero = jnp.zeros((8, 128), jnp.float32)
+        incoming = [zero]
+        for k in range(blocks - 1):
+            at_last = jnp.where(lane == first(k) + 1, 1.0, 0.0)
+            incoming.append(at_last + COUPLE * corners[1, k] * incoming[k])
+        head = [
+            jnp.where(lane == first(k), 1.0, 0.0) + COUPLE * corners[0, k] * incoming[k]
+            for k in range(blocks)
+        ]
+        carried = head[blocks - 1]
+        outgoing = [zero] * blocks
+        for k in range(blocks - 2, -1, -1):
+            outgoing[k] = carried
+            carried = head[k] + COUPLE * corners[2, k] * carried
+        picked = zero
+        even = lax.rem(sub, 2) == 0
+        for k in range(blocks):
+            value = jnp.where(even, incoming[k], outgoing[k])
+            picked = picked + jnp.where(own == k, COUPLE * value, 0.0)
+        return picked
+
+    half = lax.div(sub, 2)
+    ab_x[...] = carries(
+        lambda k: ends * (k // x_blocks) + 2 * (k % x_blocks),
+        jnp.where(half < x_blocks, col * x_blocks + half, -1),
+    )
+    ab_y[...] = carries(lambda k: 2 * planes * k + 2 * half, row + 0 * sub)
+
+    for copy in fetch:
+        copy.wait()
+    pick_row = lax.broadcasted_iota(jnp.int32, (8, cells), 0)
+    pick_lane = lax.broadcasted_iota(jnp.int32, (8, cells), 1)
+    gend[...] = jnp.zeros_like(gend)
+    for j in range(x_blocks):
+        pick = ((pick_row == 2 * j) & (pick_lane == 0)) | (
+            (pick_row == 2 * j + 1) & (pick_lane == last)
+        )
+        gend[:, j * cells : (j + 1) * cells] = dot(
+            jnp.where(pick, 1.0, 0.0), gx[j], ((1,), (1,))
+        )
+
+    wide_row = lax.broadcasted_iota(jnp.int32, (8, width), 0)
+    wide_lane = lax.broadcasted_iota(jnp.int32, (8, width), 1)
+    edge = lax.div(wide_row, 2) * cells + lax.rem(wide_row, 2) * last
+    sel_ends = jnp.where((wide_lane == edge) & (wide_row < 2 * x_blocks), 1.0, 0.0)
+    has_left, has_right = col > 0, col < cols - 1
+    sel_left = jnp.where((wide_row == tail) & (wide_lane == 0) & has_left, 1.0, 0.0)
+    sel_right = jnp.where((wide_row == 0) & (wide_lane == width - 1) & has_right, 1.0, 0.0)
+    sel_in = jnp.concatenate([sel_left, sel_right], axis=0)
+    degree_x = (
+        2.0
+        - jnp.where((wide_lane == 0) & jnp.logical_not(has_left), 1.0, 0.0)
+        - jnp.where((wide_lane == width - 1) & jnp.logical_not(has_right), 1.0, 0.0)
+    )
+    at_first, at_last = wide_lane == 0, wide_lane == width - 1
+    upper = jnp.where(row > 0, 1.0, 0.0)
+    lower = jnp.where(row < rows - 1, 1.0, 0.0)
+
+    def finish(sent):
+        for copy in sent:
+            copy.wait()
+
+    def line_rows(z):
+        return pl.ds(pl.multiple_of(z * cells, cells), cells)
+
+    finish(moves[1])
+
+    totals = []
+    for it in range(ITERS):
+        @pl.loop(0, planes)
+        def _(z):
+            h_send[it, :, line_rows(z)] = dot(sel_ends, dz[it, z, inside, :], ((1,), (1,)))
+
+        halo = [
+            send(h_send.at[it], h_recv.at[it, pl.ds(0, 8), :], h_ssem.at[it, 0], h_rsem.at[it, 0],
+                 col=lax.rem(col + 1, cols)),
+            send(h_send.at[it], h_recv.at[it, pl.ds(8, 8), :], h_ssem.at[it, 1], h_rsem.at[it, 1],
+                 col=lax.rem(col + cols - 1, cols)),
+            send(dz.at[it, :, pl.ds(cells, 8), :], dz.at[it, :, pl.ds(0, 8), :], v_ssem.at[it, 0],
+                 v_rsem.at[it, 0], row=lax.rem(row + 1, rows)),
+            send(dz.at[it, :, pl.ds(8, 8), :], dz.at[it, :, pl.ds(cells + 8, 8), :],
+                 v_ssem.at[it, 1], v_rsem.at[it, 1], row=lax.rem(row + rows - 1, rows)),
+        ]
+        if it == 0:
+            finish(moves[0])
+        finish(halo)
+
+        @pl.loop(0, planes)
+        def _(z):
+            mix[z] = dot(h_recv[it, :, line_rows(z)], sel_in, ((0,), (0,)))
+
+        @pl.loop(0, cells // 8)
+        def _(i):
+            near = pl.ds(pl.multiple_of(i * 8, 8), 24)
+            here = pl.ds(pl.multiple_of(i * 8, 8), 8)
+            y_at = wide_row + i * 8
+            top = jnp.where(y_at == 0, upper, 1.0)
+            bottom = jnp.where(y_at == last, lower, 1.0)
+            wins = [dz[it, z, near, :] for z in range(planes)]
+            mids = [w[8:16] for w in wins]
+            residual = []
+            for z in range(planes):
+                d = mids[z]
+                above = pltpu.roll(wins[z], 1, 0)[8:16]
+                below = pltpu.roll(wins[z], 23, 0)[8:16]
+                lap = top * (above - d) + bottom * (below - d)
+                lap = lap + jnp.where(at_first, 0.0, pltpu.roll(d, 1, 1))
+                lap = lap + jnp.where(at_last, 0.0, pltpu.roll(d, width - 1, 1))
+                lap = lap + mix[z, here, :] - degree_x * d
+                if z > 0:
+                    lap = lap + (mids[z - 1] - d)
+                if z < planes - 1:
+                    lap = lap + (mids[z + 1] - d)
+                e = ez[z, here, :]
+                residual.append(e - (1.0 + e) * d + KAPPA * lap)
+            for z in range(planes):
+                total = z_inv[z, 0] * residual[0]
+                for k in range(1, planes):
+                    total = total + z_inv[z, k] * residual[k]
+                mix[z, here, :] = total
+
+        @pl.loop(0, planes)
+        def _(z):
+            along = jnp.concatenate(
+                [
+                    dot(mix[z, :, j * cells : (j + 1) * cells], gx[j], ((1,), (1,)))
+                    for j in range(x_blocks)
+                ],
+                axis=1,
+            )
+            both = dot(gy[...], along, ((1,), (0,)))
+            mix[z] = both
+            x_send[it, :, line_rows(z)] = dot(sel_ends, both, ((1,), (1,)))
+
+        swaps = []
+        for o in range(1, cols):
+            swaps.append(
+                send(x_send.at[it], x_all.at[it, pl.ds(pl.multiple_of(col * 8, 8), 8), :],
+                     x_ssem.at[it, o - 1], x_rsem.at[it, o - 1], col=lax.rem(col + o, cols))
+            )
+        x_all[it, pl.ds(pl.multiple_of(col * 8, 8), 8), :] = x_send[it]
+        finish(swaps)
+
+        for z in range(planes):
+            carry = dot(ab_x[:, : cols * 8], x_all[it, :, z * cells : (z + 1) * cells], ((1,), (0,)))
+            value = mix[z] + dot(carry, gend[...], ((0,), (0,)))
+            mix[z] = value
+            y_send[it, 2 * z : 2 * z + 1, :] = value[:1]
+            y_send[it, 2 * z + 1 : 2 * z + 2, :] = value[last:]
+
+        swaps = []
+        own = pl.ds(pl.multiple_of(row * 2 * planes, 2 * planes), 2 * planes)
+        for o in range(1, rows):
+            swaps.append(
+                send(y_send.at[it], y_all.at[it, own, :], y_ssem.at[it, o - 1],
+                     y_rsem.at[it, o - 1], row=lax.rem(row + o, rows))
+            )
+        y_all[it, own, :] = y_send[it]
+        finish(swaps)
+        if it == 0:
+            finish(moves[2])
+        carry_y = dot(ab_y[:, : rows * 2 * planes], y_all[it], ((1,), (0,)))
+
+        squares = jnp.zeros((8, width), jnp.float32)
+        for z in range(planes):
+            enter, leave = carry_y[2 * z : 2 * z + 1], carry_y[2 * z + 1 : 2 * z + 2]
+
+            def settle(i, acc, z=z, enter=enter, leave=leave):
+                here = pl.ds(pl.multiple_of(i * 8, 8), 8)
+                padded = pl.ds(pl.multiple_of(i * 8 + 8, 8), 8)
+                g_first, g_last = gy[here, 0:1], gy[here, last : last + 1]
+                solved = mix[z, here, :] + g_first * enter + g_last * leave
+                d = dz[it, z, padded, :]
+                renewed = jnp.minimum(jnp.maximum(d + STEP * solved, fz[z, here, :]), 1.0)
+                dz[it + 1, z, padded, :] = renewed
+                change = renewed - d
+                return acc + change * change
+
+            squares = lax.fori_loop(0, cells // 8, settle, squares, unroll=2)
+        totals.append(jnp.sum(squares))
+
+    s_send[...] = jnp.where(sub == 0, totals[0], jnp.where(sub == 1, totals[1], 0.0))
+    final = dz.at[ITERS]
+    shares = []
+    for o in range(1, cols):
+        shares.append(
+            send(s_send, s_col.at[o - 1], sc_ssem.at[o - 1], sc_rsem.at[o - 1],
+                 col=lax.rem(col + o, cols))
+        )
+    backs = []
+    for o in range(1, cols):
+        peer = lax.rem(col + o, cols)
+        backs.append(
+            send(final.at[peer, inside, :], out.at[:, slab(col)], back_send.at[o - 1],
+                 back_recv.at[o - 1], col=peer)
+        )
+    out[:, slab(col)] = final[col, inside, :]
+    finish(shares)
+    total = s_send[...]
+    for o in range(1, cols):
+        total = total + s_col[o - 1]
+    s_row_send[...] = total
+    shares = []
+    for o in range(1, rows):
+        shares.append(
+            send(s_row_send, s_row.at[o - 1], sr_ssem.at[o - 1], sr_rsem.at[o - 1],
+                 row=lax.rem(row + o, rows))
+        )
+    finish(shares)
+    for o in range(1, rows):
+        total = total + s_row[o - 1]
+    norms[...] = jnp.sqrt(total / cell_count + EPSILON) / STEP
+    finish(backs)
+
+
+def local(energy, damage_old, crack_seeds, irreversible, line_inverses, z_inverse):
+    planes, cells, line_length = energy.shape
+    rows, cols = lax.axis_size("row"), lax.axis_size("col")
+    blocks, _, _ = line_inverses.shape
+    width = line_length // cols
+    x_blocks = width // cells
+    last = cells - 1
+    lines = cols * cells
+    shape = (rows, cols, cells, width, x_blocks, blocks, float(cols * rows * cells * line_length))
+    corners = jnp.stack(
+        [line_inverses[:, 0, 0], line_inverses[:, last, 0], line_inverses[:, 0, last]]
+    )
+    f32 = jnp.float32
+    dma = pltpu.SemaphoreType.DMA
+    vmem = pl.BlockSpec(memory_space=pltpu.VMEM)
+    smem = pl.BlockSpec(memory_space=pltpu.SMEM)
+    damage, norms = pl.pallas_call(
+        functools.partial(line_kernel, shape),
+        out_shape=(
+            jax.ShapeDtypeStruct((cells, line_length), f32),
+            jax.ShapeDtypeStruct((8, 128), f32),
+        ),
+        in_specs=[smem, smem, vmem, vmem, vmem, vmem, pl.BlockSpec(memory_space=pl.ANY)],
+        out_specs=(vmem, vmem),
+        scratch_shapes=[
+            pltpu.VMEM((cells, line_length), f32),
+            pltpu.VMEM((cells, line_length), f32),
+            pltpu.VMEM((cols, cells, width), f32),
+            pltpu.VMEM((cols, cells, width), f32),
+            pltpu.VMEM((ITERS + 1, cols, cells + 16, width), f32),
+            pltpu.VMEM((cols, cells, width), f32),
+            pltpu.VMEM((x_blocks, cells, cells), f32),
+            pltpu.VMEM((cells, cells), f32),
+            pltpu.VMEM((8, width), f32),
+            pltpu.VMEM((8, 128), f32),
+            pltpu.VMEM((8, 128), f32),
+            pltpu.VMEM((ITERS, 8, lines), f32),
+            pltpu.VMEM((ITERS, 8 * cols, lines), f32),
+            pltpu.VMEM((ITERS, 8, lines), f32),
+            pltpu.VMEM((ITERS, 16, lines), f32),
+            pltpu.VMEM((ITERS, 2 * cols, width), f32),
+            pltpu.VMEM((ITERS, 2 * cols * rows, width), f32),
+            pltpu.VMEM((8, 128), f32),
+            pltpu.VMEM((cols - 1, 8, 128), f32),
+            pltpu.VMEM((8, 128), f32),
+            pltpu.VMEM((rows - 1, 8, 128), f32),
+            dma((x_blocks + 1,)),
+            dma((3, cols - 1)),
+            dma((3, cols - 1)),
+            dma((cols - 1,)),
+            dma((cols - 1,)),
+            dma((ITERS, cols - 1)),
+            dma((ITERS, cols - 1)),
+            dma((ITERS, 2)),
+            dma((ITERS, 2)),
+            dma((ITERS, 2)),
+            dma((ITERS, 2)),
+            dma((ITERS, rows - 1)),
+            dma((ITERS, rows - 1)),
+            dma((cols - 1,)),
+            dma((cols - 1,)),
+            dma((rows - 1,)),
+            dma((rows - 1,)),
+        ],
+        compiler_params=pltpu.CompilerParams(
+            has_side_effects=True, vmem_limit_bytes=60 * 1024 * 1024
+        ),
+        name="line_iterations",
+    )(
+        corners,
+        z_inverse,
+        energy[0],
+        damage_old[0],
+        crack_seeds[0],
+        irreversible[0],
+        line_inverses,
+    )
+    return damage[None], norms[:ITERS, 0]
+
+
 def solution(mesh):
+    def local_any(energy, damage_old, crack_seeds, irreversible, line_inverses, z_inverse):
+        rows, cols = mesh.shape["row"], mesh.shape["col"]
+        block_cells = line_inverses.shape[1]
+        width = energy.shape[2] // cols
+        whole_blocks = (
+            energy.shape[0] == 1
+            and energy.shape[1] == block_cells
+            and width % block_cells == 0
+            and 2 * (width // block_cells) <= 8
+            and 2 * cols == 8
+            and 8 * max(rows, cols) <= 128
+            and min(rows, cols) > 2
+        )
+        chosen = local if whole_blocks else local_turned
+        return chosen(energy, damage_old, crack_seeds, irreversible, line_inverses, z_inverse)
+
     return jax.shard_map(
-        local,
+        local_any,
         mesh=mesh,
         in_specs=(
             P("col", "row", None),

time: 748 us -> 184 us (0.25); the launches traced: 739 us -> 184 us
  waiting for transfers between devices: 205 us -> 0 us
  Pallas kernels: 0 us -> 177 us
  blocking collectives: 174 us -> 0 us
  local copies, waits for them, and re-layouts: 174 us -> 5.44 us
  other arithmetic: 110 us -> 0.59 us
  starting transfers between devices: 42.7 us -> 0 us
  matrix products: 24 us -> 0 us
  between operations: 9.81 us -> 0.64 us
    all_to_all x9 -> x0, waiting for transfers between devices: 205 us -> none  [the longest x2 76.3 us: local(): lax.all_to_all(jnp.swapaxes(partial_value, 1, 2), 'row', split_axis=1, co...]
    pallas_call x0 -> x1, Pallas kernels: none -> 177 us  [local(): pl.pallas_call(functools.partial(line_kernel, shape), out_shape=(jax.Shap...]
    all_to_all x3 -> x0, blocking collectives: 136 us -> none  [the longest x2 107 us: local(): lax.all_to_all(along_z, 'row', split_axis=2, concat_axis=1, tiled=True)]
    unnamed x54 -> x1, local copies, waits for them, and re-layouts: 81.7 us -> 3.13 us
    all_to_all x11 -> x0, local copies, waits for them, and re-layouts: 45 us -> none  [the longest x4 18 us: local(): lax.all_to_all(jnp.swapaxes(partial_value, 1, 2), 'row', split_axis=1, co...]
    all_to_all x9 -> x0, starting transfers between devices: 42.7 us -> none  [the longest x2 10.7 us: local(): lax.all_to_all(jnp.swapaxes(damage, 1, 2), 'row', split_axis=1, concat_ax...]
    psum x1 -> x0, blocking collectives: 37.3 us -> none  [local(): global_sums = lax.psum(jnp.stack(own_sums), ('row', 'col'))]
    dot_general x6 -> x0, matrix products: 24 us -> none  [the longest x2 13.5 us: local(): jnp.einsum('zk,kxy->zxy', z_inverse, along_y, precision=lax.Precision.HIG...]
  transfers between devices with their start and end apart: 9 -> 0, of which waited for: 9 -> 0; matrix products, arithmetic and copies ran while one was open for 14% -> 0% of each run, Pallas kernels for 0% -> 0%
where the time goes in v1:
time: 184 us
  Pallas kernels  177 us (96%)
  local copies, waits for them, and re-layouts  5.44 us (3%)
    pallas_call x1, Pallas kernels, local(): pl.pallas_call(functools.partial(line_kernel, shape), out_shape=(jax.Shap...  177 us

profile of v1, /device:TPU:0, one launch (start us, length us, event | category | flops | bytes accessed | tf_op | source)
XLA Modules:
  0.0 183.9 jit_solution(7002141677189060450)
XLA Ops:
  0.6 1.0 slice_reduce_fusion.2
  1.6 0.6 pad_maximum_fusion.corners
  2.2 177.2 %line_iterations.1 = (f32[256,2048]{1,0:T(8,128)}, f32[8,128]{1,0:T(8,128)}) custom-call(f32[3,8]{1,0:T(4,128)} %pad_maximum_fusion.corners, f32[4,4]{1,0:T(4,128)} %z_inv.1, f32[256,2048]{1,0:T(8,128)} %bitcast.8, f32[256,2048]{1,0:T(8,128)} %bitcast.9, s32[256,2048]{1,0:T(8,128)} %bitcast.10, s32[256,2048]{1,0:T(8,128)} %bitcast.11, f32[8,256,256]{2,1,0:T(8,128)} %inverses.1), custom_call_target="tpu_custom_call" | custom-call | tf_op jit(solution)/shard_map/line_iterations/pallas_call | solution.py:473
  179.4 1.3 slice_reduce_fusion.3
  180.8 3.1 %copy.9 = f32[1,256,2048]{2,1,0:T(8,128)} copy(f32[1,256,2048]{2,1,0:T(8,128)} %bitcast.12) | data formatting | bytes 4194304

commit v2 on v1

--- a/solution.py
+++ b/solution.py
@@ -130,12 +130,15 @@
     corners,
     z_inv,
     energy,
+    damage_hbm,
+    seeds_hbm,
+    irreversible_hbm,
+    inverses,
+    out,
+    norms,
     damage_old,
     crack_seeds,
     irreversible,
-    inverses,
-    out,
-    norms,
     start,
     bound,
     ez,
@@ -144,6 +147,11 @@
     mix,
     gx,
     gy,
+    gx_high,
+    gx_low,
+    gy_high,
+    gy_low,
+    h_in,
     gend,
     ab_x,
     ab_y,
@@ -180,7 +188,7 @@
     last = cells - 1
     row, col = lax.axis_index("row"), lax.axis_index("col")
     ends = 8
-    tail = 2 * x_blocks - 1
+    tail = 8 - x_blocks
 
     def slab(who):
         return pl.ds(pl.multiple_of(who * width, width), width)
@@ -197,29 +205,63 @@
         return lax.dot_general(
             a, b, (contract, ((), ())), precision=HIGHEST, preferred_element_type=jnp.float32
         )
+
+    def split(a):
+        high = a.astype(jnp.bfloat16)
+        return high, (a - high.astype(jnp.float32)).astype(jnp.bfloat16)
+
+    def dot3(a, b):
+        def part(u, v):
+            return jnp.dot(u, v, preferred_element_type=jnp.float32)
+
+        return part(a[0], b[0]) + (part(a[0], b[1]) + part(a[1], b[0]))
+
+    def line_ends(field):
+        tile_lane = lax.broadcasted_iota(jnp.int32, (cells, 128), 1)
+        packed = field[:, :128]
+        for j in range(x_blocks):
+            head = field[:, j * cells : j * cells + 128]
+            end = field[:, (j + 1) * cells - 128 : (j + 1) * cells]
+            if j > 0:
+                head = pltpu.roll(head, j, 1)
+                end = pltpu.roll(end, 128 - j, 1)
+            packed = jnp.where(tile_lane == j, head, packed)
+            packed = jnp.where(tile_lane == 127 - j, end, packed)
+        turned = packed.T
+        at = lax.broadcasted_iota(jnp.int32, (8, cells), 0)
+        kept = (at < x_blocks) | (at >= 8 - x_blocks)
+        return jnp.where(kept, jnp.where(at < x_blocks, turned[:8], turned[120:]), 0.0)
 
     fetch = [
         pltpu.make_async_copy(inverses.at[col * x_blocks + j], gx.at[j], local_sems.at[j])
         for j in range(x_blocks)
     ]
     fetch.append(pltpu.make_async_copy(inverses.at[row], gy, local_sems.at[x_blocks]))
-    for copy in fetch:
-        copy.start()
+    pulls = [
+        pltpu.make_async_copy(damage_hbm, damage_old, local_sems.at[x_blocks + 1]),
+        pltpu.make_async_copy(seeds_hbm, crack_seeds, local_sems.at[x_blocks + 2]),
+        pltpu.make_async_copy(irreversible_hbm, irreversible, local_sems.at[x_blocks + 3]),
+        pltpu.make_async_copy(energy.at[:, slab(col)], ez.at[col], local_sems.at[x_blocks + 4]),
+    ]
 
     moves = []
     inside = pl.ds(8, cells)
 
-    def move(index, src, landing):
+    def move(index, src, landing, part=slice(None)):
         sent = []
         for o in range(1, cols):
             peer = lax.rem(col + o, cols)
             sent.append(
-                send(src.at[:, slab(peer)], landing, move_send.at[index, o - 1],
+                send(src.at[part, slab(peer)], landing, move_send.at[index, o - 1],
                      move_recv.at[index, o - 1], col=peer)
             )
         moves.append(sent)
 
     move(0, energy, ez.at[col])
+    for copy in pulls + fetch:
+        copy.start()
+    for copy in pulls:
+        copy.wait()
 
     @pl.loop(0, cells // 16)
     def _(i):
@@ -229,20 +271,18 @@
         start[at, :] = jnp.where(seeded, 1.0, old)
         bound[at, :] = jnp.where(seeded, 1.0, jnp.where(irreversible[at, :] == 1, old, 0.0))
 
-    ez[col] = energy[:, slab(col)]
     move(1, start, dz.at[0, col, inside, :])
     dz[0, col, inside, :] = start[:, slab(col)]
-    move(2, bound, fz.at[col])
     fz[col] = bound[:, slab(col)]
 
     lane = lax.broadcasted_iota(jnp.int32, (8, 128), 1)
     sub = lax.broadcasted_iota(jnp.int32, (8, 128), 0)
 
-    def carries(first, own):
+    def carries(first, final, own):
         zero = jnp.zeros((8, 128), jnp.float32)
         incoming = [zero]
         for k in range(blocks - 1):
-            at_last = jnp.where(lane == first(k) + 1, 1.0, 0.0)
+            at_last = jnp.where(lane == final(k), 1.0, 0.0)
             incoming.append(at_last + COUPLE * corners[1, k] * incoming[k])
         head = [
             jnp.where(lane == first(k), 1.0, 0.0) + COUPLE * corners[0, k] * incoming[k]
@@ -262,32 +302,30 @@
 
     half = lax.div(sub, 2)
     ab_x[...] = carries(
-        lambda k: ends * (k // x_blocks) + 2 * (k % x_blocks),
+        lambda k: ends * (k // x_blocks) + k % x_blocks,
+        lambda k: ends * (k // x_blocks) + 7 - k % x_blocks,
         jnp.where(half < x_blocks, col * x_blocks + half, -1),
     )
-    ab_y[...] = carries(lambda k: 2 * planes * k + 2 * half, row + 0 * sub)
+    ab_y[...] = carries(
+        lambda k: 2 * planes * k + 2 * half,
+        lambda k: 2 * planes * k + 2 * half + 1,
+        row + 0 * sub,
+    )
 
     for copy in fetch:
         copy.wait()
-    pick_row = lax.broadcasted_iota(jnp.int32, (8, cells), 0)
-    pick_lane = lax.broadcasted_iota(jnp.int32, (8, cells), 1)
     gend[...] = jnp.zeros_like(gend)
     for j in range(x_blocks):
-        pick = ((pick_row == 2 * j) & (pick_lane == 0)) | (
-            (pick_row == 2 * j + 1) & (pick_lane == last)
-        )
-        gend[:, j * cells : (j + 1) * cells] = dot(
-            jnp.where(pick, 1.0, 0.0), gx[j], ((1,), (1,))
-        )
+        turned = gx[j].T
+        gx_high[j], gx_low[j] = split(turned)
+        block = slice(j * cells, (j + 1) * cells)
+        gend[2 * j : 2 * j + 1, block] = turned[:1]
+        gend[2 * j + 1 : 2 * j + 2, block] = turned[last:]
+    gy_high[...], gy_low[...] = split(gy[...])
 
     wide_row = lax.broadcasted_iota(jnp.int32, (8, width), 0)
     wide_lane = lax.broadcasted_iota(jnp.int32, (8, width), 1)
-    edge = lax.div(wide_row, 2) * cells + lax.rem(wide_row, 2) * last
-    sel_ends = jnp.where((wide_lane == edge) & (wide_row < 2 * x_blocks), 1.0, 0.0)
     has_left, has_right = col > 0, col < cols - 1
-    sel_left = jnp.where((wide_row == tail) & (wide_lane == 0) & has_left, 1.0, 0.0)
-    sel_right = jnp.where((wide_row == 0) & (wide_lane == width - 1) & has_right, 1.0, 0.0)
-    sel_in = jnp.concatenate([sel_left, sel_right], axis=0)
     degree_x = (
         2.0
         - jnp.where((wide_lane == 0) & jnp.logical_not(has_left), 1.0, 0.0)
@@ -310,7 +348,7 @@
     for it in range(ITERS):
         @pl.loop(0, planes)
         def _(z):
-            h_send[it, :, line_rows(z)] = dot(sel_ends, dz[it, z, inside, :], ((1,), (1,)))
+            h_send[it, :, line_rows(z)] = line_ends(dz[it, z, inside, :])
 
         halo = [
             send(h_send.at[it], h_recv.at[it, pl.ds(0, 8), :], h_ssem.at[it, 0], h_rsem.at[it, 0],
@@ -324,11 +362,18 @@
         ]
         if it == 0:
             finish(moves[0])
+            pieces = [slice(0, cells // 2), slice(cells // 2, cells)]
+            move(2, bound, fz.at[col, pieces[0], :], pieces[0])
         finish(halo)
 
         @pl.loop(0, planes)
         def _(z):
-            mix[z] = dot(h_recv[it, :, line_rows(z)], sel_in, ((0,), (0,)))
+            left = h_recv[it, tail : tail + 1, line_rows(z)]
+            right = h_recv[it, 8:9, line_rows(z)]
+            at = lax.broadcasted_iota(jnp.int32, (128, cells), 0)
+            left = jnp.where((at == 0) & has_left, left, 0.0)
+            right = jnp.where((at == 127) & has_right, right, 0.0)
+            h_in[z] = (left + right).T
 
         @pl.loop(0, cells // 8)
         def _(i):
@@ -347,7 +392,10 @@
                 lap = top * (above - d) + bottom * (below - d)
                 lap = lap + jnp.where(at_first, 0.0, pltpu.roll(d, 1, 1))
                 lap = lap + jnp.where(at_last, 0.0, pltpu.roll(d, width - 1, 1))
-                lap = lap + mix[z, here, :] - degree_x * d
+                edges = h_in[z, here, :]
+                lap = lap + jnp.where(at_first, jnp.tile(edges, (1, width // 128)), 0.0)
+                lap = lap + jnp.where(at_last, jnp.tile(edges, (1, width // 128)), 0.0)
+                lap = lap - degree_x * d
                 if z > 0:
                     lap = lap + (mids[z - 1] - d)
                 if z < planes - 1:
@@ -364,14 +412,16 @@
         def _(z):
             along = jnp.concatenate(
                 [
-                    dot(mix[z, :, j * cells : (j + 1) * cells], gx[j], ((1,), (1,)))
+                    dot3(
+                        split(mix[z, :, j * cells : (j + 1) * cells]), (gx_high[j], gx_low[j])
+                    )
                     for j in range(x_blocks)
                 ],
                 axis=1,
             )
-            both = dot(gy[...], along, ((1,), (0,)))
+            both = dot3((gy_high[...], gy_low[...]), split(along))
             mix[z] = both
-            x_send[it, :, line_rows(z)] = dot(sel_ends, both, ((1,), (1,)))
+            x_send[it, :, line_rows(z)] = line_ends(both)
 
         swaps = []
         for o in range(1, cols):
@@ -380,6 +430,8 @@
                      x_ssem.at[it, o - 1], x_rsem.at[it, o - 1], col=lax.rem(col + o, cols))
             )
         x_all[it, pl.ds(pl.multiple_of(col * 8, 8), 8), :] = x_send[it]
+        if it == 0:
+            move(3, bound, fz.at[col, pieces[1], :], pieces[1])
         finish(swaps)
 
         for z in range(planes):
@@ -399,7 +451,7 @@
         y_all[it, own, :] = y_send[it]
         finish(swaps)
         if it == 0:
-            finish(moves[2])
+            finish(moves[2] + moves[3])
         carry_y = dot(ab_y[:, : rows * 2 * planes], y_all[it], ((1,), (0,)))
 
         squares = jnp.zeros((8, width), jnp.float32)
@@ -476,9 +528,12 @@
             jax.ShapeDtypeStruct((cells, line_length), f32),
             jax.ShapeDtypeStruct((8, 128), f32),
         ),
-        in_specs=[smem, smem, vmem, vmem, vmem, vmem, pl.BlockSpec(memory_space=pl.ANY)],
+        in_specs=[smem, smem] + [pl.BlockSpec(memory_space=pl.ANY)] * 5,
         out_specs=(vmem, vmem),
         scratch_shapes=[
+            pltpu.VMEM((cells, line_length), f32),
+            pltpu.VMEM((cells, line_length), jnp.int32),
+            pltpu.VMEM((cells, line_length), jnp.int32),
             pltpu.VMEM((cells, line_length), f32),
             pltpu.VMEM((cells, line_length), f32),
             pltpu.VMEM((cols, cells, width), f32),
@@ -487,6 +542,11 @@
             pltpu.VMEM((cols, cells, width), f32),
             pltpu.VMEM((x_blocks, cells, cells), f32),
             pltpu.VMEM((cells, cells), f32),
+            pltpu.VMEM((x_blocks, cells, cells), jnp.bfloat16),
+            pltpu.VMEM((x_blocks, cells, cells), jnp.bfloat16),
+            pltpu.VMEM((cells, cells), jnp.bfloat16),
+            pltpu.VMEM((cells, cells), jnp.bfloat16),
+            pltpu.VMEM((cols, cells, 128), f32),
             pltpu.VMEM((8, width), f32),
             pltpu.VMEM((8, 128), f32),
             pltpu.VMEM((8, 128), f32),
@@ -500,9 +560,9 @@
             pltpu.VMEM((cols - 1, 8, 128), f32),
             pltpu.VMEM((8, 128), f32),
             pltpu.VMEM((rows - 1, 8, 128), f32),
-            dma((x_blocks + 1,)),
-            dma((3, cols - 1)),
-            dma((3, cols - 1)),
+            dma((x_blocks + 5,)),
+            dma((4, cols - 1)),
+            dma((4, cols - 1)),
             dma((cols - 1,)),
             dma((cols - 1,)),
             dma((ITERS, cols - 1)),

time: 184 us -> 154 us (0.84)
  Pallas kernels: 177 us -> 147 us
    pallas_call x1, Pallas kernels: 177 us -> 147 us  [local(): pl.pallas_call(functools.partial(line_kernel, shape), out_shape=(jax.Shap...]
where the time goes in v2:
time: 154 us
  Pallas kernels  147 us (95%)
  local copies, waits for them, and re-layouts  5.44 us (4%)
    pallas_call x1, Pallas kernels, local(): pl.pallas_call(functools.partial(line_kernel, shape), out_shape=(jax.Shap...  147 us
    unnamed x1, local copies, waits for them, and re-layouts  3.13 us

profile of v2, /device:TPU:0, one launch (start us, length us, event | category | flops | bytes accessed | tf_op | source)
XLA Modules:
  0.0 153.6 jit_solution(13320919263304789843)
XLA Ops:
  0.6 1.0 slice_reduce_fusion.2
  1.6 0.6 pad_maximum_fusion.corners
  2.2 146.9 %line_iterations.1 = (f32[256,2048]{1,0:T(8,128)}, f32[8,128]{1,0:T(8,128)}) custom-call(f32[3,8]{1,0:T(4,128)} %pad_maximum_fusion.corners, f32[4,4]{1,0:T(4,128)} %z_inv.1, f32[256,2048]{1,0:T(8,128)} %bitcast.8, f32[256,2048]{1,0:T(8,128)} %bitcast.9, s32[256,2048]{1,0:T(8,128)} %bitcast.10, s32[256,2048]{1,0:T(8,128)} %bitcast.11, f32[8,256,256]{2,1,0:T(8,128)} %inverses.1), custom_call_target="tpu_custom_call" | custom-call | tf_op jit(solution)/shard_map/line_iterations/pallas_call | solution.py:525
  149.2 1.3 slice_reduce_fusion.3
  150.5 3.1 %copy.9 = f32[1,256,2048]{2,1,0:T(8,128)} copy(f32[1,256,2048]{2,1,0:T(8,128)} %bitcast.12) | data formatting | bytes 4194304

commit v3 on v2

--- a/solution.py
+++ b/solution.py
@@ -201,10 +201,12 @@
         copy.start()
         return copy
 
-    def dot(a, b, contract):
-        return lax.dot_general(
-            a, b, (contract, ((), ())), precision=HIGHEST, preferred_element_type=jnp.float32
-        )
+    def weighted(weights, field, kept):
+        total = None
+        for n in kept:
+            term = weights[:, n : n + 1] * field[n : n + 1]
+            total = term if total is None else total + term
+        return total
 
     def split(a):
         high = a.astype(jnp.bfloat16)
@@ -435,8 +437,19 @@
         finish(swaps)
 
         for z in range(planes):
-            carry = dot(ab_x[:, : cols * 8], x_all[it, :, z * cells : (z + 1) * cells], ((1,), (0,)))
-            value = mix[z] + dot(carry, gend[...], ((0,), (0,)))
+            kept = [
+                ends * c + n for c in range(cols) for n in range(ends)
+                if n < x_blocks or n >= ends - x_blocks
+            ]
+            carry = weighted(ab_x[...], x_all[it, :, z * cells : (z + 1) * cells], kept)
+            carry = jnp.concatenate([carry, jnp.zeros((120, cells), jnp.float32)], axis=0).T
+            parts = []
+            for j in range(x_blocks):
+                block = slice(j * cells, (j + 1) * cells)
+                enter = carry[:, 2 * j : 2 * j + 1] * gend[2 * j : 2 * j + 1, block]
+                leave = carry[:, 2 * j + 1 : 2 * j + 2] * gend[2 * j + 1 : 2 * j + 2, block]
+                parts.append(mix[z, :, block] + enter + leave)
+            value = jnp.concatenate(parts, axis=1)
             mix[z] = value
             y_send[it, 2 * z : 2 * z + 1, :] = value[:1]
             y_send[it, 2 * z + 1 : 2 * z + 2, :] = value[last:]
@@ -452,7 +465,7 @@
         finish(swaps)
         if it == 0:
             finish(moves[2] + moves[3])
-        carry_y = dot(ab_y[:, : rows * 2 * planes], y_all[it], ((1,), (0,)))
+        carry_y = weighted(ab_y[...], y_all[it], range(rows * 2 * planes))
 
         squares = jnp.zeros((8, width), jnp.float32)
         for z in range(planes):

time: 154 us -> 153 us (level)
  no operation moved by 1% of the time
where the time goes in v3:
time: 153 us; the launch traced here: 152 us
  Pallas kernels  146 us (95%)
  local copies, waits for them, and re-layouts  5.44 us (4%)
    pallas_call x1, Pallas kernels, local(): pl.pallas_call(functools.partial(line_kernel, shape), out_shape=(jax.Shap...  146 us
    unnamed x1, local copies, waits for them, and re-layouts  3.13 us

profile of v3, /device:TPU:0, one launch (start us, length us, event | category | flops | bytes accessed | tf_op | source)
XLA Modules:
  0.0 152.4 jit_solution(13866483624588286445)
XLA Ops:
  0.6 1.0 slice_reduce_fusion.2
  1.6 0.6 pad_maximum_fusion.corners
  2.2 145.7 %line_iterations.1 = (f32[256,2048]{1,0:T(8,128)}, f32[8,128]{1,0:T(8,128)}) custom-call(f32[3,8]{1,0:T(4,128)} %pad_maximum_fusion.corners, f32[4,4]{1,0:T(4,128)} %z_inv.1, f32[256,2048]{1,0:T(8,128)} %bitcast.8, f32[256,2048]{1,0:T(8,128)} %bitcast.9, s32[256,2048]{1,0:T(8,128)} %bitcast.10, s32[256,2048]{1,0:T(8,128)} %bitcast.11, f32[8,256,256]{2,1,0:T(8,128)} %inverses.1), custom_call_target="tpu_custom_call" | custom-call | tf_op jit(solution)/shard_map/line_iterations/pallas_call | solution.py:538
  148.0 1.3 slice_reduce_fusion.3
  149.3 3.1 %copy.9 = f32[1,256,2048]{2,1,0:T(8,128)} copy(f32[1,256,2048]{2,1,0:T(8,128)} %bitcast.12) | data formatting | bytes 4194304
